TPU v7x, 256 devices: a 8x8x2 block of a 8x8x16 slice. The times are simulated.
256 devices in a mesh: groups: 2 (over z), blk: 64 (over x, y), head: 2 (over core).
Axes of the slice: x: 8, y: 8, z: 2, core: 2. Of those that a mesh axis runs over, the one named last changes fastest.
The devices are a block of a 8x8x16 slice.
Arguments:
- q_latent: float32 [256, 128, 512], P(('groups', 'blk'), 'head'), parts along dimension 0, may hold values from -16 to 16
- q_rope: float32 [256, 128, 64], P(('groups', 'blk'), 'head'), parts along dimension 0, may hold values from -8 to 8
- cache_latent: float32 [262144, 512], P(('groups', 'blk')), parts along dimension 0, may hold values from -8 to 8
- cache_rope: float32 [262144, 64], P(('groups', 'blk')), parts along dimension 0, may hold values from -4 to 4
- home_offset: int32 [256], P(('groups', 'blk')), parts along dimension 0, may hold values from 0 to 14335
- lengths: int32 [256], P(('groups', 'blk')), parts along dimension 0, may hold values from 1 to 14336, as said below
Outputs:
- attended: float32 [256, 128, 512], P(('groups', 'blk'), 'head'), parts along dimension 0
There are 2 independent parts, one for each index of `groups`. A program takes and returns all parts, laid end to end along the dimension named above; each array names one. Nothing has to cross between parts.
Inputs may be any that keep to these rules, and one draw needn't show every extreme that they name: `lengths`: some query has all 14336 cells live.
All inputs are finite; a program needn't handle non-finite values.
Results may differ from a plain program's by a relative error of at most 0.0003.
Values sent between devices are 32-bit elements; how exact they have to be, the bound alone decides.
No kernel may reach another device: no remote copies, remote signals or barrier semaphores. Data moves between devices by JAX's collectives and lax.ppermute only.
A program may use at most 64 MiB of HBM per device.

v0:
```python
import functools
import math

import jax
import jax.numpy as jnp
from jax import lax
from jax.experimental import pallas as pl
from jax.experimental.pallas import tpu as pltpu
from jax.sharding import PartitionSpec as P

ROPE = 64
NOPE = 128
HOPS = 3
TILE = 512

SCALE = math.log2(math.e) / math.sqrt(NOPE + ROPE)
DEAD = -1e30
FLOOR = -1e29
MIB = 1024 * 1024
F32 = jnp.float32
BF16 = jnp.bfloat16

VMEM = pl.BlockSpec(memory_space=pltpu.VMEM)
SMEM = pl.BlockSpec(memory_space=pltpu.SMEM)


def call(body, outs, in_specs, args, flops, scratch=(), limit=24):
    nbytes = sum(math.prod(o.shape) * o.dtype.itemsize for o in outs)
    nbytes += sum(math.prod(a.shape) * a.dtype.itemsize for a in args)
    return pl.pallas_call(
        body,
        out_shape=outs,
        in_specs=in_specs,
        out_specs=[VMEM] * len(outs),
        scratch_shapes=list(scratch),
        compiler_params=pltpu.CompilerParams(vmem_limit_bytes=limit * MIB),
        cost_estimate=pl.CostEstimate(flops=flops, bytes_accessed=nbytes, transcendentals=0),
    )(*args)


def two_parts(x):
    high = x.astype(BF16)
    return high, (x - high.astype(F32)).astype(BF16)


def pack_body(home_ref, lengths_ref, latent_ref, rope_ref, out_ref):
    count, heads, width = latent_ref.shape
    rows = count * heads
    rope = rope_ref.shape[2]
    out_ref[0:width, :] = latent_ref[...].reshape(rows, width).T * SCALE
    flat = rope_ref[...].reshape(rows, rope)
    flat = jnp.concatenate([flat, jnp.zeros((rows, 128 - rope), F32)], axis=1)
    out_ref[width : width + rope, :] = flat.T[0:rope, :] * SCALE
    query = lax.broadcasted_iota(jnp.int32, (8, rows), 1) // heads
    which = lax.broadcasted_iota(jnp.int32, (8, rows), 0)
    home = jnp.zeros((8, rows), jnp.int32)
    extent = jnp.zeros((8, rows), jnp.int32)
    for q in range(count):
        home = jnp.where(query == q, home_ref[q], home)
        extent = jnp.where(query == q, lengths_ref[q], extent)
    out_ref[width + rope :, :] = jnp.where(which == 0, home, extent).astype(F32)


def pack(q_latent, q_rope, home_offset, lengths):
    count, heads, width = q_latent.shape
    rows = width + q_rope.shape[2] + 8
    out = [jax.ShapeDtypeStruct((rows, count * heads), F32)]
    return call(
        pack_body, out, [SMEM, SMEM, VMEM, VMEM], (home_offset, lengths, q_latent, q_rope), 1000
    )[0]


def prepare_body(latent_ref, rope_ref, ch_ref, cl_ref, th_ref, tl_ref, kr_ref):
    cells, width = latent_ref.shape
    rope = rope_ref.shape[0]

    def step(i, _):
        at = pl.ds(pl.multiple_of(i * 256, 256), 256)
        high, low = two_parts(latent_ref[at, :])
        ch_ref[at, :] = high
        cl_ref[at, :] = low
        th_ref[:, at] = high.T
        tl_ref[:, at] = low.T
        keys = jnp.concatenate([rope_ref[:, at], jnp.zeros((128 - rope, 256), F32)], axis=0).T
        high, low = two_parts(keys[:, 0:rope])
        kr_ref[at, :] = jnp.concatenate([high, low, high, low], axis=1)
        return 0

    lax.fori_loop(0, cells // 256, step, 0)


def prepare(cache_latent, cache_rope):
    cells, width = cache_latent.shape
    rope = cache_rope.shape[1]
    outs = [
        jax.ShapeDtypeStruct((cells, width), BF16),
        jax.ShapeDtypeStruct((cells, width), BF16),
        jax.ShapeDtypeStruct((width, cells), BF16),
        jax.ShapeDtypeStruct((width, cells), BF16),
        jax.ShapeDtypeStruct((cells, 4 * rope), BF16),
    ]
    return call(prepare_body, outs, [VMEM, VMEM], (cache_latent, cache_rope.T), 10**9, limit=32)


def attend_body(slots, *refs):
    n = len(slots)
    packs, rest = refs[:n], refs[n:]
    ch_ref, cl_ref, th_ref, tl_ref, kr_ref = rest[:5]
    outs, scores_ref = rest[5 : 5 + n], rest[5 + n]
    cells, width = ch_ref.shape
    rope = kr_ref.shape[1] // 4
    window = (2 * HOPS + 1) * cells
    rows = packs[0].shape[1]
    total_rows = n * rows

    def joined(lo, hi):
        return jnp.concatenate([p[lo:hi, :] for p in packs], axis=1)

    qh, ql = two_parts(joined(0, width))
    rh, rl = two_parts(joined(width, width + rope))
    qr = jnp.concatenate([rh, rh, rl, rl], axis=0)
    meta = joined(width + rope, width + rope + 8).astype(jnp.int32)
    first = meta[0:1, :] - jnp.concatenate(
        [jnp.full((1, rows), s * cells, jnp.int32) for s in slots], axis=1
    )
    extent = meta[1:2, :]

    def score(i, top):
        at = pl.ds(pl.multiple_of(i * TILE, TILE), TILE)
        high = ch_ref[at, :]
        s = (
            jnp.dot(high, qh, preferred_element_type=F32)
            + jnp.dot(high, ql, preferred_element_type=F32)
            + jnp.dot(cl_ref[at, :], qh, preferred_element_type=F32)
            + jnp.dot(kr_ref[at, :], qr, preferred_element_type=F32)
        )
        cell = lax.broadcasted_iota(jnp.int32, (TILE, total_rows), 0) + i * TILE
        offset = cell - first
        offset = jnp.where(offset < 0, offset + window, offset)
        s = jnp.where(offset < extent, s, DEAD)
        scores_ref[at, :] = s
        return jnp.maximum(top, jnp.max(s, axis=0, keepdims=True))

    start = jnp.full((1, total_rows), FLOOR, F32)
    peak = lax.fori_loop(0, cells // TILE, score, start)

    def weigh(i, carry):
        total, summed = carry
        at = pl.ds(pl.multiple_of(i * TILE, TILE), TILE)
        weights = jnp.exp2(scores_ref[at, :] - peak)
        total = total + jnp.sum(weights, axis=0, keepdims=True)
        wh, wl = two_parts(weights)
        product = (
            jnp.dot(th_ref[:, at], wh, preferred_element_type=F32)
            + jnp.dot(th_ref[:, at], wl, preferred_element_type=F32)
            + jnp.dot(tl_ref[:, at], wh, preferred_element_type=F32)
        )
        for k in range(n):
            outs[k][0:width, :] += product[:, k * rows : (k + 1) * rows]
        return total, summed

    for k in range(n):
        outs[k][0:width, :] = jnp.zeros((width, rows), F32)
    total, _ = lax.fori_loop(0, cells // TILE, weigh, (jnp.zeros((1, total_rows), F32), 0))
    for k in range(n):
        at = slice(k * rows, (k + 1) * rows)
        outs[k][width:, :] = jnp.concatenate(
            [peak[:, at], total[:, at], jnp.zeros((6, rows), F32)], axis=0
        )


def attend(packs, slots, prepared):
    n = len(packs)
    cells, width = prepared[0].shape
    rows = packs[0].shape[1]
    outs = [jax.ShapeDtypeStruct((width + 8, rows), F32)] * n
    return call(
        functools.partial(attend_body, tuple(slots)),
        outs,
        [VMEM] * (n + 5),
        tuple(packs) + tuple(prepared),
        2 * 6 * 128 * n * cells * 1088,
        scratch=[pltpu.VMEM((cells, n * rows), F32)],
    )


def merged(parts, width):
    peaks = [p[width : width + 1, :] for p in parts]
    peak = functools.reduce(jnp.maximum, peaks)
    scales = [jnp.exp2(x - peak) for x in peaks]
    total = sum(p[width + 1 : width + 2, :] * s for p, s in zip(parts, scales))
    summed = sum(p[0:width, :] * s for p, s in zip(parts, scales))
    return peak, total, summed


def merge_body(*refs):
    half = len(refs) // 3
    for k in range(half):
        a, b, out = refs[k], refs[half + k], refs[2 * half + k]
        width, rows = out.shape[0] - 8, out.shape[1]
        peak, total, summed = merged([a, b], width)
        out[0:width, :] = summed
        out[width:, :] = jnp.concatenate([peak, total, jnp.zeros((6, rows), F32)], axis=0)


def merge(left, right):
    outs = [jax.ShapeDtypeStruct(x.shape, F32) for x in left]
    args = tuple(left) + tuple(right)
    return call(merge_body, outs, [VMEM] * len(args), args, 10**6)


def finish_body(a_ref, b_ref, c_ref, out_ref):
    count, heads, width = out_ref.shape
    _, total, summed = merged([a_ref, b_ref, c_ref], width)
    out_ref[...] = (summed / total).T.reshape(count, heads, width)


def finish(own, upper, lower, shape):
    out = [jax.ShapeDtypeStruct(shape, F32)]
    return call(finish_body, out, [VMEM] * 3, (own, upper, lower), 10**6)[0]


def shift(x, by):
    size = lax.axis_size("blk")
    return lax.ppermute(x, "blk", [(i, (i + by) % size) for i in range(size)])


def shards(q_latent, q_rope, cache_latent, cache_rope, home_offset, lengths):
    own = pack(q_latent, q_rope, home_offset, lengths)
    up, down = shift(own, 1), shift(own, -1)
    prepared = prepare(cache_latent, cache_rope)
    here = attend([own], [HOPS], prepared)[0]
    partial = []
    for hop in range(1, HOPS + 1):
        held = (up, down)
        if hop < HOPS:
            up, down = shift(up, 1), shift(down, -1)
        partial.append(attend(held, [HOPS + hop, HOPS - hop], prepared))
    back = partial[-1]
    for hop in range(HOPS, 0, -1):
        back = [shift(back[0], -1), shift(back[1], 1)]
        if hop > 1:
            back = merge(back, partial[hop - 2])
    return finish(here, back[0], back[1], q_latent.shape)


def solution(mesh):
    return jax.shard_map(
        shards,
        mesh=mesh,
        in_specs=(
            P(("groups", "blk"), "head", None),
            P(("groups", "blk"), "head", None),
            P(("groups", "blk"), None),
            P(("groups", "blk"), None),
            P(("groups", "blk")),
            P(("groups", "blk")),
        ),
        out_specs=P(("groups", "blk"), "head", None),
        check_vma=False,
    )
```

profile of v0, /device:TPU:528, one launch (start us, length us, event | category | flops | bytes accessed | tf_op | source)
XLA Modules:
  0.0 95.9 jit_solution(3826907439091086298)
XLA Ops:
  0.0 0.0 copy-start.2
  0.0 0.9 copy-done.2
  1.0 0.0 copy-start.3
  1.0 0.8 copy-done.3
  1.8 0.0 copy-start.4
  1.8 0.7 copy-done.4
  2.4 0.0 copy-start.5
  2.4 0.7 copy-done.5
  3.1 0.7 shard_map.64.refs_0_
  3.8 2.9 %collective-permute-start = (f32[584,128]{1,0:T(8,128)S(1)}, f32[584,128]{1,0:T(8,128)S(1)}, u32[]{:S(2)}, u32[]{:S(2)}) collective-permute-start(f32[584,128]{1,0:T(8,128)S(1)} %shard_map.64.refs_0_), channel_id=1, source_target_pairs={{0,2},{2,4},{4,6},{6,8},{8,10},{10,12},{12,14},{14,16},{16,18},{18... | collective-permute-start | bytes 897032 | tf_op jit(solution)/shard_map/ppermute | solution.py:225
  6.7 15.6 %collective-permute-start.3 = (f32[584,128]{1,0:T(8,128)S(1)}, f32[584,128]{1,0:T(8,128)S(1)}, u32[]{:S(2)}, u32[]{:S(2)}) collective-permute-start(f32[584,128]{1,0:T(8,128)S(1)} %shard_map.64.refs_0_), channel_id=1, source_target_pairs={{0,126},{2,0},{4,2},{6,4},{8,6},{10,8},{12,10},{14,12},{16,14},{18... | collective-permute-start | bytes 897032 | tf_op jit(solution)/shard_map/ppermute | solution.py:225
  22.3 7.1 %collective-permute-done.refs_0_ = f32[584,128]{1,0:T(8,128)S(1)} collective-permute-done((f32[584,128]{1,0:T(8,128)S(1)}, f32[584,128]{1,0:T(8,128)S(1)}, u32[]{:S(2)}, u32[]{:S(2)}) %collective-permute-start) | collective-permute-done | bytes 299040 | tf_op jit(solution)/shard_map/ppermute | solution.py:225
  29.3 0.0 collective-permute-start.1
  29.3 0.0 collective-permute-done.3.refs_1_
  29.3 5.1 %collective-permute-start.4 = (f32[584,128]{1,0:T(8,128)S(1)}, f32[584,128]{1,0:T(8,128)S(1)}, u32[]{:S(2)}, u32[]{:S(2)}) collective-permute-start(f32[584,128]{1,0:T(8,128)S(1)} %collective-permute-done.3.refs_1_), channel_id=1, source_target_pairs={{0,126},{2,0},{4,2},{6,4},{8,6},{10,8},{12,10},{14,12},{16,14},{18... | collective-permute-start | bytes 897032 | tf_op jit(solution)/shard_map/ppermute | solution.py:225
  34.4 6.3 %collective-permute-done.1.refs_0_ = f32[584,128]{1,0:T(8,128)S(1)} collective-permute-done((f32[584,128]{1,0:T(8,128)S(1)}, f32[584,128]{1,0:T(8,128)S(1)}, u32[]{:S(2)}, u32[]{:S(2)}) %collective-permute-start.1) | collective-permute-done | bytes 299040 | tf_op jit(solution)/shard_map/ppermute | solution.py:225
  40.7 0.0 collective-permute-start.2
  40.7 0.0 collective-permute-done.4.refs_1_
  40.7 5.1 %collective-permute-start.5 = (f32[584,128]{1,0:T(8,128)S(1)}, f32[584,128]{1,0:T(8,128)S(1)}, u32[]{:S(2)}, u32[]{:S(2)}) collective-permute-start(f32[584,128]{1,0:T(8,128)S(1)} %collective-permute-done.4.refs_1_), channel_id=1, source_target_pairs={{0,126},{2,0},{4,2},{6,4},{8,6},{10,8},{12,10},{14,12},{16,14},{18... | collective-permute-start | bytes 897032 | tf_op jit(solution)/shard_map/ppermute | solution.py:225
  45.8 0.0 copy-start
  45.8 2.2 %copy-done = f32[2048,512]{1,0:T(8,128)S(1)} copy-done((f32[2048,512]{1,0:T(8,128)S(1)}, f32[2048,512]{1,0:T(8,128)}, u32[]{:S(2)}) %copy-start) | copy-done | bytes 4194328
  48.0 0.0 copy-start.1
  48.0 1.0 %copy-done.1 = f32[2048,64]{0,1:T(8,128)S(1)} copy-done((f32[2048,64]{0,1:T(8,128)S(1)}, f32[2048,64]{0,1:T(8,128)}, u32[]{:S(2)}) %copy-start.1) | copy-done | bytes 524312
  49.0 2.8 %shard_map.65 = (bf16[2048,512]{1,0:T(8,128)(2,1)S(1)}, bf16[2048,512]{1,0:T(8,128)(2,1)S(1)}, bf16[512,2048]{1,0:T(8,128)(2,1)S(1)}, bf16[512,2048]{1,0:T(8,128)(2,1)S(1)}, bf16[2048,256]{1,0:T(8,128)(2,1)S(1)}) custom-call(f32[2048,512]{1,0:T(8,128)S(1)} %copy-done, f32[64,2048]{1,0:T(8,128)S(1)} %bitcast.1), custom_call_target="tpu_custom_call" | custom-call | flops 1000000000 | bytes 14155776 | tf_op jit(solution)/shard_map/pallas_call | solution.py:30
  51.8 0.0 collective-permute-done.2.refs_0_
  51.8 0.0 collective-permute-done.5.refs_1_
  51.8 5.3 %shard_map.67 = (f32[520,128]{1,0:T(8,128)S(1)}, f32[520,128]{1,0:T(8,128)S(1)}) custom-call(f32[584,128]{1,0:T(8,128)S(1)} %collective-permute-done.2.refs_0_, f32[584,128]{1,0:T(8,128)S(1)} %collective-permute-done.5.refs_1_, bf16[2048,512]{1,0:T(8,128)(2,1)S(1)} %get-tuple-element.20.refs_1_.refs_2_, ...), custom_call_target="tpu_custom_call" | custom-call | flops 6845104128 | bytes 10567680 | tf_op jit(solution)/shard_map/pallas_call | solution.py:30
  57.2 5.5 %collective-permute-start.6 = (f32[520,128]{1,0:T(8,128)S(1)}, f32[520,128]{1,0:T(8,128)S(1)}, u32[]{:S(2)}, u32[]{:S(2)}) collective-permute-start(f32[520,128]{1,0:T(8,128)S(1)} %get-tuple-element.25), channel_id=1, source_target_pairs={{0,126},{2,0},{4,2},{6,4},{8,6},{10,8},{12,10},{14,12},{16,14},{18... | collective-permute-start | bytes 798728 | tf_op jit(solution)/shard_map/ppermute | solution.py:225
  62.6 0.0 collective-permute-start.7
  62.6 5.3 %shard_map.68 = (f32[520,128]{1,0:T(8,128)S(1)}, f32[520,128]{1,0:T(8,128)S(1)}) custom-call(f32[584,128]{1,0:T(8,128)S(1)} %collective-permute-done.1.refs_0_, f32[584,128]{1,0:T(8,128)S(1)} %collective-permute-done.4.refs_1_, bf16[2048,512]{1,0:T(8,128)(2,1)S(1)} %get-tuple-element.20.refs_1_.refs_2_, ...), custom_call_target="tpu_custom_call" | custom-call | flops 6845104128 | bytes 10567680 | tf_op jit(solution)/shard_map/pallas_call | solution.py:30
  68.0 0.6 collective-permute-done.6.refs_0_
  68.6 3.5 %collective-permute-done.7.refs_1_ = f32[520,128]{1,0:T(8,128)S(1)} collective-permute-done((f32[520,128]{1,0:T(8,128)S(1)}, f32[520,128]{1,0:T(8,128)S(1)}, u32[]{:S(2)}, u32[]{:S(2)}) %collective-permute-start.7) | collective-permute-done | bytes 266272 | tf_op jit(solution)/shard_map/ppermute | solution.py:225
  72.1 0.1 shard_map.69
  72.2 5.5 %collective-permute-start.8 = (f32[520,128]{1,0:T(8,128)S(1)}, f32[520,128]{1,0:T(8,128)S(1)}, u32[]{:S(2)}, u32[]{:S(2)}) collective-permute-start(f32[520,128]{1,0:T(8,128)S(1)} %get-tuple-element.29), channel_id=1, source_target_pairs={{0,126},{2,0},{4,2},{6,4},{8,6},{10,8},{12,10},{14,12},{16,14},{18... | collective-permute-start | bytes 798728 | tf_op jit(solution)/shard_map/ppermute | solution.py:225
  77.7 0.0 collective-permute-start.9
  77.7 5.3 %shard_map.70 = (f32[520,128]{1,0:T(8,128)S(1)}, f32[520,128]{1,0:T(8,128)S(1)}) custom-call(f32[584,128]{1,0:T(8,128)S(1)} %collective-permute-done.refs_0_, f32[584,128]{1,0:T(8,128)S(1)} %collective-permute-done.3.refs_1_, bf16[2048,512]{1,0:T(8,128)(2,1)S(1)} %get-tuple-element.20.refs_1_.refs_2_, ...), custom_call_target="tpu_custom_call" | custom-call | flops 6845104128 | bytes 10567680 | tf_op jit(solution)/shard_map/pallas_call | solution.py:30
  83.0 0.0 collective-permute-done.8.refs_0_
  83.0 1.1 %collective-permute-done.9.refs_1_ = f32[520,128]{1,0:T(8,128)S(1)} collective-permute-done((f32[520,128]{1,0:T(8,128)S(1)}, f32[520,128]{1,0:T(8,128)S(1)}, u32[]{:S(2)}, u32[]{:S(2)}) %collective-permute-start.9) | collective-permute-done | bytes 266272 | tf_op jit(solution)/shard_map/ppermute | solution.py:225
  84.1 0.1 shard_map.71
  84.2 4.4 %collective-permute-start.10 = (f32[520,128]{1,0:T(8,128)S(1)}, f32[520,128]{1,0:T(8,128)S(1)}, u32[]{:S(2)}, u32[]{:S(2)}) collective-permute-start(f32[520,128]{1,0:T(8,128)S(1)} %get-tuple-element.33), channel_id=1, source_target_pairs={{0,126},{2,0},{4,2},{6,4},{8,6},{10,8},{12,10},{14,12},{16,14},{18... | collective-permute-start | bytes 798728 | tf_op jit(solution)/shard_map/ppermute | solution.py:225
  88.6 0.0 collective-permute-start.11
  88.6 5.1 %shard_map.66.a_ref = f32[520,128]{1,0:T(8,128)S(1)} custom-call(f32[584,128]{1,0:T(8,128)S(1)} %shard_map.64.refs_0_, bf16[2048,512]{1,0:T(8,128)(2,1)S(1)} %get-tuple-element.20.refs_1_.refs_2_, bf16[2048,512]{1,0:T(8,128)(2,1)S(1)} %get-tuple-element.21.refs_2_.refs_3_, bf16[512,2048]{1,0:T(8,128)(2,1)S(1)} %get-tuple-element.22.refs_3_.refs_4_, ...), custom_call_target="tpu_custom_call" | custom-call | flops 3422552064 | bytes 10002432 | tf_op jit(solution)/shard_map/pallas_call | solution.py:30
  93.7 0.0 collective-permute-done.10.b_ref
  93.7 1.3 %collective-permute-done.11.c_ref = f32[520,128]{1,0:T(8,128)S(1)} collective-permute-done((f32[520,128]{1,0:T(8,128)S(1)}, f32[520,128]{1,0:T(8,128)S(1)}, u32[]{:S(2)}, u32[]{:S(2)}) %collective-permute-start.11) | collective-permute-done | bytes 266272 | tf_op jit(solution)/shard_map/ppermute | solution.py:225
  95.0 0.9 shard_map.72
Async XLA Ops:
  0.0 0.9 copy-start.2
  1.0 0.8 copy-start.3
  1.8 0.7 copy-start.4
  2.4 0.7 copy-start.5
  3.8 25.5 %collective-permute-start = (f32[584,128]{1,0:T(8,128)S(1)}, f32[584,128]{1,0:T(8,128)S(1)}, u32[]{:S(2)}, u32[]{:S(2)}) collective-permute-start(f32[584,128]{1,0:T(8,128)S(1)} %shard_map.64.refs_0_), channel_id=1, source_target_pairs={{0,2},{2,4},{4,6},{6,8},{8,10},{10,12},{12,14},{14,16},{16,18},{18... | collective-permute-start | bytes 897032 | tf_op jit(solution)/shard_map/ppermute | solution.py:225
  6.7 22.7 %collective-permute-start.3 = (f32[584,128]{1,0:T(8,128)S(1)}, f32[584,128]{1,0:T(8,128)S(1)}, u32[]{:S(2)}, u32[]{:S(2)}) collective-permute-start(f32[584,128]{1,0:T(8,128)S(1)} %shard_map.64.refs_0_), channel_id=1, source_target_pairs={{0,126},{2,0},{4,2},{6,4},{8,6},{10,8},{12,10},{14,12},{16,14},{18... | collective-permute-start | bytes 897032 | tf_op jit(solution)/shard_map/ppermute | solution.py:225
  29.3 11.4 %collective-permute-start.1 = (f32[584,128]{1,0:T(8,128)S(1)}, f32[584,128]{1,0:T(8,128)S(1)}, u32[]{:S(2)}, u32[]{:S(2)}) collective-permute-start(f32[584,128]{1,0:T(8,128)S(1)} %collective-permute-done.refs_0_), channel_id=1, source_target_pairs={{0,2},{2,4},{4,6},{6,8},{8,10},{10,12},{12,14},{14,16},{16,18},{18... | collective-permute-start | bytes 897032 | tf_op jit(solution)/shard_map/ppermute | solution.py:225
  29.3 11.4 %collective-permute-start.4 = (f32[584,128]{1,0:T(8,128)S(1)}, f32[584,128]{1,0:T(8,128)S(1)}, u32[]{:S(2)}, u32[]{:S(2)}) collective-permute-start(f32[584,128]{1,0:T(8,128)S(1)} %collective-permute-done.3.refs_1_), channel_id=1, source_target_pairs={{0,126},{2,0},{4,2},{6,4},{8,6},{10,8},{12,10},{14,12},{16,14},{18... | collective-permute-start | bytes 897032 | tf_op jit(solution)/shard_map/ppermute | solution.py:225
  40.7 11.1 %collective-permute-start.2 = (f32[584,128]{1,0:T(8,128)S(1)}, f32[584,128]{1,0:T(8,128)S(1)}, u32[]{:S(2)}, u32[]{:S(2)}) collective-permute-start(f32[584,128]{1,0:T(8,128)S(1)} %collective-permute-done.1.refs_0_), channel_id=1, source_target_pairs={{0,2},{2,4},{4,6},{6,8},{8,10},{10,12},{12,14},{14,16},{16,18},{18... | collective-permute-start | bytes 897032 | tf_op jit(solution)/shard_map/ppermute | solution.py:225
  40.7 11.1 %collective-permute-start.5 = (f32[584,128]{1,0:T(8,128)S(1)}, f32[584,128]{1,0:T(8,128)S(1)}, u32[]{:S(2)}, u32[]{:S(2)}) collective-permute-start(f32[584,128]{1,0:T(8,128)S(1)} %collective-permute-done.4.refs_1_), channel_id=1, source_target_pairs={{0,126},{2,0},{4,2},{6,4},{8,6},{10,8},{12,10},{14,12},{16,14},{18... | collective-permute-start | bytes 897032 | tf_op jit(solution)/shard_map/ppermute | solution.py:225
  45.8 2.2 %copy-start = (f32[2048,512]{1,0:T(8,128)S(1)}, f32[2048,512]{1,0:T(8,128)}, u32[]{:S(2)}) copy-start(f32[2048,512]{1,0:T(8,128)} %latent_ref.3) | copy-start | bytes 12582916
  48.0 1.0 %copy-start.1 = (f32[2048,64]{0,1:T(8,128)S(1)}, f32[2048,64]{0,1:T(8,128)}, u32[]{:S(2)}) copy-start(f32[2048,64]{0,1:T(8,128)} %param.9) | copy-start | bytes 1572868
  57.2 11.4 %collective-permute-start.6 = (f32[520,128]{1,0:T(8,128)S(1)}, f32[520,128]{1,0:T(8,128)S(1)}, u32[]{:S(2)}, u32[]{:S(2)}) collective-permute-start(f32[520,128]{1,0:T(8,128)S(1)} %get-tuple-element.25), channel_id=1, source_target_pairs={{0,126},{2,0},{4,2},{6,4},{8,6},{10,8},{12,10},{14,12},{16,14},{18... | collective-permute-start | bytes 798728 | tf_op jit(solution)/shard_map/ppermute | solution.py:225
  62.6 9.5 %collective-permute-start.7 = (f32[520,128]{1,0:T(8,128)S(1)}, f32[520,128]{1,0:T(8,128)S(1)}, u32[]{:S(2)}, u32[]{:S(2)}) collective-permute-start(f32[520,128]{1,0:T(8,128)S(1)} %get-tuple-element.26), channel_id=1, source_target_pairs={{0,2},{2,4},{4,6},{6,8},{8,10},{10,12},{12,14},{14,16},{16,18},{18... | collective-permute-start | bytes 798728 | tf_op jit(solution)/shard_map/ppermute | solution.py:225
  72.2 10.8 %collective-permute-start.8 = (f32[520,128]{1,0:T(8,128)S(1)}, f32[520,128]{1,0:T(8,128)S(1)}, u32[]{:S(2)}, u32[]{:S(2)}) collective-permute-start(f32[520,128]{1,0:T(8,128)S(1)} %get-tuple-element.29), channel_id=1, source_target_pairs={{0,126},{2,0},{4,2},{6,4},{8,6},{10,8},{12,10},{14,12},{16,14},{18... | collective-permute-start | bytes 798728 | tf_op jit(solution)/shard_map/ppermute | solution.py:225
  77.7 6.4 %collective-permute-start.9 = (f32[520,128]{1,0:T(8,128)S(1)}, f32[520,128]{1,0:T(8,128)S(1)}, u32[]{:S(2)}, u32[]{:S(2)}) collective-permute-start(f32[520,128]{1,0:T(8,128)S(1)} %get-tuple-element.30), channel_id=1, source_target_pairs={{0,2},{2,4},{4,6},{6,8},{8,10},{10,12},{12,14},{14,16},{16,18},{18... | collective-permute-start | bytes 798728 | tf_op jit(solution)/shard_map/ppermute | solution.py:225
  84.2 9.5 %collective-permute-start.10 = (f32[520,128]{1,0:T(8,128)S(1)}, f32[520,128]{1,0:T(8,128)S(1)}, u32[]{:S(2)}, u32[]{:S(2)}) collective-permute-start(f32[520,128]{1,0:T(8,128)S(1)} %get-tuple-element.33), channel_id=1, source_target_pairs={{0,126},{2,0},{4,2},{6,4},{8,6},{10,8},{12,10},{14,12},{16,14},{18... | collective-permute-start | bytes 798728 | tf_op jit(solution)/shard_map/ppermute | solution.py:225
  88.6 6.4 %collective-permute-start.11 = (f32[520,128]{1,0:T(8,128)S(1)}, f32[520,128]{1,0:T(8,128)S(1)}, u32[]{:S(2)}, u32[]{:S(2)}) collective-permute-start(f32[520,128]{1,0:T(8,128)S(1)} %get-tuple-element.34), channel_id=1, source_target_pairs={{0,2},{2,4},{4,6},{6,8},{8,10},{10,12},{12,14},{14,16},{16,18},{18... | collective-permute-start | bytes 798728 | tf_op jit(solution)/shard_map/ppermute | solution.py:225
where the time goes:
time: 96.2 us; the launch traced here: 95.9 us
  starting transfers between devices  43.9 us (46%)
  Pallas kernels  25.6 us (27%)
  waiting for transfers between devices  20 us (21%)
  local copies, waits for them, and re-layouts  6.33 us (7%)
    ppermute x12, starting transfers between devices, shift(): return lax.ppermute(x, 'blk', [(i, (i + by) % size) for i in range(size)])  43.9 us
    pallas_call x9, Pallas kernels, call(): pl.pallas_call(body, out_shape=outs, in_specs=in_specs, out_specs=[VMEM]...  25.6 us
    ppermute x12, waiting for transfers between devices, shift(): return lax.ppermute(x, 'blk', [(i, (i + by) % size) for i in range(size)])  20 us
    unnamed x12, local copies, waits for them, and re-layouts  6.33 us
  transfers between devices with their start and end apart: 12, of which 6 were waited for; matrix products, arithmetic and copies ran while one was open for 0% of the time, Pallas kernels for 19%

commit v1 on v0

v1 whole, which is shorter than its diff:
```python
import functools
import math

import jax
import jax.numpy as jnp
from jax import lax
from jax.experimental import pallas as pl
from jax.experimental.pallas import tpu as pltpu
from jax.sharding import PartitionSpec as P


ROPE = 64
NOPE = 128
HOPS = 3
TILE = 1024

SCALE = math.log2(math.e) / math.sqrt(NOPE + ROPE)
DEAD = -1e30
FLOOR = -1e29
MIB = 1024 * 1024
F32 = jnp.float32
BF16 = jnp.bfloat16

VMEM = pl.BlockSpec(memory_space=pltpu.VMEM)
HBM = pl.BlockSpec(memory_space=pltpu.HBM)


def call(body, outs, in_specs, args, flops, scratch=(), limit=24):
    nbytes = sum(math.prod(o.shape) * o.dtype.itemsize for o in outs)
    nbytes += sum(math.prod(a.shape) * a.dtype.itemsize for a in args)
    return pl.pallas_call(
        body,
        out_shape=outs,
        in_specs=in_specs,
        out_specs=[VMEM] * len(outs),
        scratch_shapes=list(scratch),
        compiler_params=pltpu.CompilerParams(vmem_limit_bytes=limit * MIB),
        cost_estimate=pl.CostEstimate(flops=flops, bytes_accessed=nbytes, transcendentals=0),
    )(*args)


def dot(a, b):
    return jnp.dot(a, b, preferred_element_type=F32)


def two_parts(x):
    high = x.astype(BF16)
    return high, (x - high.astype(F32)).astype(BF16)


def pack_body(home_hbm, lengths_hbm, latent_hbm, rope_hbm, out_ref, home_ref, lengths_ref, latent_ref, rope_ref, sems):
    moves = [
        pltpu.make_async_copy(src, dst, sems.at[k])
        for k, (src, dst) in enumerate(
            [
                (latent_hbm, latent_ref),
                (rope_hbm, rope_ref),
                (home_hbm, home_ref),
                (lengths_hbm, lengths_ref),
            ]
        )
    ]
    for move in moves:
        move.start()
    for move in moves:
        move.wait()
    count, heads, width = latent_ref.shape
    rows = count * heads
    rope = rope_ref.shape[2]
    out_ref[0:width, :] = latent_ref[...].reshape(rows, width).T * SCALE
    flat = rope_ref[...].reshape(rows, rope)
    flat = jnp.concatenate([flat, jnp.zeros((rows, 128 - rope), F32)], axis=1)
    out_ref[width : width + rope, :] = flat.T[0:rope, :] * SCALE
    query = lax.broadcasted_iota(jnp.int32, (8, rows), 1) // heads
    which = lax.broadcasted_iota(jnp.int32, (8, rows), 0)
    home = jnp.zeros((8, rows), jnp.int32)
    extent = jnp.zeros((8, rows), jnp.int32)
    for q in range(count):
        home = jnp.where(query == q, home_ref[q], home)
        extent = jnp.where(query == q, lengths_ref[q], extent)
    out_ref[width + rope :, :] = jnp.where(which == 0, home, extent).astype(F32)


def pack(q_latent, q_rope, home_offset, lengths):
    count, heads, width = q_latent.shape
    rows = width + q_rope.shape[2] + 8
    out = [jax.ShapeDtypeStruct((rows, count * heads), F32)]
    scratch = [
        pltpu.SMEM(home_offset.shape, jnp.int32),
        pltpu.SMEM(lengths.shape, jnp.int32),
        pltpu.VMEM(q_latent.shape, F32),
        pltpu.VMEM(q_rope.shape, F32),
        pltpu.SemaphoreType.DMA((4,)),
    ]
    args = (home_offset, lengths, q_latent, q_rope)
    return call(pack_body, out, [HBM] * 4, args, 1000, scratch, limit=57)[0]


def prepare_body(latent_hbm, rope_hbm, ch_ref, cl_ref, th_ref, tl_ref, kr_ref, latent_ref, rope_ref, sems):
    cells = latent_hbm.shape[0]
    rope = rope_hbm.shape[0]
    piece = 256
    moves = [pltpu.make_async_copy(rope_hbm, rope_ref, sems.at[cells // piece])]
    for i in range(cells // piece):
        at = pl.ds(i * piece, piece)
        moves.append(pltpu.make_async_copy(latent_hbm.at[at], latent_ref.at[at], sems.at[i]))
    for move in moves:
        move.start()
    moves[0].wait()
    for i in range(cells // piece):
        at = slice(i * piece, (i + 1) * piece)
        moves[i + 1].wait()
        high, low = two_parts(latent_ref[at, :])
        ch_ref[at, :] = high
        cl_ref[at, :] = low
        th_ref[:, at] = high.T
        tl_ref[:, at] = low.T
        keys = jnp.concatenate([rope_ref[:, at], jnp.zeros((128 - rope, piece), F32)], axis=0).T
        high, low = two_parts(keys[:, 0:rope])
        kr_ref[at, :] = jnp.concatenate([high, low, high, low], axis=1)


def prepare(cache_latent, cache_rope):
    cells, width = cache_latent.shape
    rope = cache_rope.shape[1]
    outs = [
        jax.ShapeDtypeStruct((cells, width), BF16),
        jax.ShapeDtypeStruct((cells, width), BF16),
        jax.ShapeDtypeStruct((width, cells), BF16),
        jax.ShapeDtypeStruct((width, cells), BF16),
        jax.ShapeDtypeStruct((cells, 4 * rope), BF16),
    ]
    scratch = [
        pltpu.VMEM(cache_latent.shape, F32),
        pltpu.VMEM((rope, cells), F32),
        pltpu.SemaphoreType.DMA((cells // 256 + 1,)),
    ]
    args = (cache_latent, cache_rope.T)
    return call(prepare_body, outs, [HBM] * 2, args, 10**9, scratch, limit=44)


def attend_body(hop, sides, *refs):
    n = len(sides)
    packs, rest = refs[:n], refs[n:]
    ch_ref, cl_ref, th_ref, tl_ref, kr_ref = rest[:5]
    outs, scores_ref = rest[5 : 5 + n], rest[5 + n]
    cells, width = ch_ref.shape
    rope = kr_ref.shape[1] // 4
    window = (2 * HOPS + 1) * cells
    rows = packs[0].shape[1]
    total_rows = n * rows

    def joined(lo, hi):
        return jnp.concatenate([p[lo:hi, :] for p in packs], axis=1)

    def times_both(left, high, low):
        if n > 1:
            return dot(left, high) + dot(left, low)
        both = dot(left, jnp.concatenate([high, low], axis=1))
        return both[:, :total_rows] + both[:, total_rows:]

    qh, ql = two_parts(joined(0, width))
    rh, rl = two_parts(joined(width, width + rope))
    qr = jnp.concatenate([rh, rh, rl, rl], axis=0)
    meta = joined(width + rope, width + rope + 8).astype(jnp.int32)
    place = 1 - 2 * lax.rem(lax.axis_index("blk"), 2)
    slots = [HOPS - hop * place * side for side in sides]
    first = meta[0:1, :] - jnp.concatenate(
        [jnp.full((1, rows), s * cells, jnp.int32) for s in slots], axis=1
    )
    extent = meta[1:2, :]

    def score(i, top):
        at = pl.ds(pl.multiple_of(i * TILE, TILE), TILE)
        s = (
            times_both(ch_ref[at, :], qh, ql)
            + dot(cl_ref[at, :], qh)
            + dot(kr_ref[at, :], qr)
        )
        cell = lax.broadcasted_iota(jnp.int32, (TILE, total_rows), 0) + i * TILE
        offset = cell - first
        offset = jnp.where(offset < 0, offset + window, offset)
        s = jnp.where(offset < extent, s, DEAD)
        scores_ref[at, :] = s
        return jnp.maximum(top, jnp.max(s, axis=0, keepdims=True))

    start = jnp.full((1, total_rows), FLOOR, F32)
    peak = lax.fori_loop(0, cells // TILE, score, start)

    def weigh(i, total):
        at = pl.ds(pl.multiple_of(i * TILE, TILE), TILE)
        weights = jnp.exp2(scores_ref[at, :] - peak)
        wh, wl = two_parts(weights)
        product = times_both(th_ref[:, at], wh, wl) + dot(tl_ref[:, at], wh)
        for k in range(n):
            outs[k][0:width, :] += product[:, k * rows : (k + 1) * rows]
        return total + jnp.sum(weights, axis=0, keepdims=True)

    for k in range(n):
        outs[k][0:width, :] = jnp.zeros((width, rows), F32)
    total = lax.fori_loop(0, cells // TILE, weigh, jnp.zeros((1, total_rows), F32))
    for k in range(n):
        at = slice(k * rows, (k + 1) * rows)
        outs[k][width:, :] = jnp.concatenate(
            [peak[:, at], total[:, at], jnp.zeros((6, rows), F32)], axis=0
        )


def attend(packs, hop, sides, prepared):
    n = len(packs)
    cells, width = prepared[0].shape
    rows = packs[0].shape[1]
    outs = [jax.ShapeDtypeStruct((width + 8, rows), F32)] * n
    return call(
        functools.partial(attend_body, hop, sides),
        outs,
        [VMEM] * (n + 5),
        tuple(packs) + tuple(prepared),
        2 * 6 * 128 * n * cells * 1088,
        scratch=[pltpu.VMEM((cells, n * rows), F32)],
    )


def merged(parts, width):
    peaks = [p[width : width + 1, :] for p in parts]
    peak = functools.reduce(jnp.maximum, peaks)
    scales = [jnp.exp2(x - peak) for x in peaks]
    total = sum(p[width + 1 : width + 2, :] * s for p, s in zip(parts, scales))
    summed = sum(p[0:width, :] * s for p, s in zip(parts, scales))
    return peak, total, summed


def merge_body(a, b, out):
    width, rows = out.shape[0] - 8, out.shape[1]
    peak, total, summed = merged([a, b], width)
    out[0:width, :] = summed
    out[width:, :] = jnp.concatenate([peak, total, jnp.zeros((6, rows), F32)], axis=0)


def merge(left, right):
    outs = [jax.ShapeDtypeStruct(left.shape, F32)]
    return call(merge_body, outs, [VMEM] * 2, (left, right), 10**6)[0]


def finish_body(a_ref, b_ref, c_ref, out_ref):
    count, heads, width = out_ref.shape
    _, total, summed = merged([a_ref, b_ref, c_ref], width)
    out_ref[...] = (summed / total).T.reshape(count, heads, width)


def finish(own, upper, lower, shape):
    out = [jax.ShapeDtypeStruct(shape, F32)]
    return call(finish_body, out, [VMEM] * 3, (own, upper, lower), 10**6)[0]


def swap(x, parity):
    size = lax.axis_size("blk")
    pairs = []
    for i in range(parity, size + parity, 2):
        pairs += [(i % size, (i + 1) % size), ((i + 1) % size, i % size)]
    return lax.ppermute(x, "blk", pairs)


def shards(q_latent, q_rope, cache_latent, cache_rope, home_offset, lengths):
    own = pack(q_latent, q_rope, home_offset, lengths)
    even, odd = swap(own, 0), swap(own, 1)
    prepared = prepare(cache_latent, cache_rope)
    evens, odds = [even], [odd]
    for _ in range(2, HOPS + 1):
        even, odd = (swap(odds[-1], 0), swap(evens[-1], 1))
        evens.append(even)
        odds.append(odd)
    partial = [
        attend([evens[hop - 1], odds[hop - 1]], hop, (1, -1), prepared)
        for hop in range(1, HOPS)
    ]
    even = attend([even], HOPS, (1,), prepared)[0]
    odd = attend([odd], HOPS, (-1,), prepared)[0]
    here = attend([own], 0, (1,), prepared)[0]
    for hop in range(HOPS, 0, -1):
        even, odd = swap(even, 0), swap(odd, 1)
        if hop > 1:
            even, odd = merge(odd, partial[hop - 2][0]), merge(even, partial[hop - 2][1])
    return finish(here, even, odd, q_latent.shape)


def solution(mesh):
    return jax.shard_map(
        shards,
        mesh=mesh,
        in_specs=(
            P(("groups", "blk"), "head", None),
            P(("groups", "blk"), "head", None),
            P(("groups", "blk"), None),
            P(("groups", "blk"), None),
            P(("groups", "blk")),
            P(("groups", "blk")),
        ),
        out_specs=P(("groups", "blk"), "head", None),
        check_vma=False,
    )
```

time: 96.2 us -> 82.4 us (0.86)
  the two profiles are of different devices: /device:TPU:528 before, /device:TPU:640 now
where the time goes in v1:
time: 82.4 us; the launch traced here: 82.2 us
  starting transfers between devices  40.4 us (49%)
  Pallas kernels  25.6 us (31%)
  waiting for transfers between devices  15 us (18%)
  local copies, waits for them, and re-layouts  1.05 us (1%)
    ppermute x12, starting transfers between devices, swap(): return lax.ppermute(x, 'blk', pairs)  40.4 us
    pallas_call x12, Pallas kernels, call(): pl.pallas_call(body, out_shape=outs, in_specs=in_specs, out_specs=[VMEM]...  25.6 us
    ppermute x12, waiting for transfers between devices, swap(): return lax.ppermute(x, 'blk', pairs)  15 us
  transfers between devices with their start and end apart: 12, of which 4 were waited for; matrix products, arithmetic and copies ran while one was open for 0% of the time, Pallas kernels for 28%

profile of v1, /device:TPU:640, one launch (start us, length us, event | category | flops | bytes accessed | tf_op | source)
XLA Modules:
  0.0 82.2 jit_solution(6122416163635282018)
XLA Ops:
  0.0 1.9 %shard_map.64.refs_0_ = f32[584,128]{1,0:T(8,128)} custom-call(s32[2]{0:T(128)} %home_hbm.1, s32[2]{0:T(128)} %lengths_hbm.1, f32[2,64,512]{2,1,0:T(8,128)} %latent_hbm.2, f32[2,64,64]{2,1,0:T(8,128)} %rope_hbm.1), custom_call_target="tpu_custom_call" | custom-call | flops 1000 | bytes 593936 | tf_op jit(solution)/shard_map/pallas_call | solution.py:31
  1.9 2.9 %collective-permute-start = (f32[584,128]{1,0:T(8,128)}, f32[584,128]{1,0:T(8,128)S(1)}, u32[]{:S(2)}, u32[]{:S(2)}) collective-permute-start(f32[584,128]{1,0:T(8,128)} %shard_map.64.refs_0_), channel_id=1, source_target_pairs={{0,2},{2,0},{4,6},{6,4},{8,10},{10,8},{12,14},{14,12},{16,18},{18,... | collective-permute-start | bytes 897032 | tf_op jit(solution)/shard_map/ppermute | solution.py:261
  4.8 12.5 %collective-permute-start.4 = (f32[584,128]{1,0:T(8,128)}, f32[584,128]{1,0:T(8,128)S(1)}, u32[]{:S(2)}, u32[]{:S(2)}) collective-permute-start(f32[584,128]{1,0:T(8,128)} %shard_map.64.refs_0_), channel_id=1, source_target_pairs={{2,4},{4,2},{6,8},{8,6},{10,12},{12,10},{14,16},{16,14},{18,20},{2... | collective-permute-start | bytes 897032 | tf_op jit(solution)/shard_map/ppermute | solution.py:261
  17.3 0.0 collective-permute-done.refs_0_
  17.3 9.0 %collective-permute-start.1 = (f32[584,128]{1,0:T(8,128)S(1)}, f32[584,128]{1,0:T(8,128)S(1)}, u32[]{:S(2)}, u32[]{:S(2)}) collective-permute-start(f32[584,128]{1,0:T(8,128)S(1)} %collective-permute-done.refs_0_), channel_id=1, source_target_pairs={{2,4},{4,2},{6,8},{8,6},{10,12},{12,10},{14,16},{16,14},{18,20},{2... | collective-permute-start | bytes 897032 | tf_op jit(solution)/shard_map/ppermute | solution.py:261
  26.2 0.0 collective-permute-done.4.refs_1_
  26.2 0.0 collective-permute-start.5
  26.2 6.3 %collective-permute-done.1.refs_1_ = f32[584,128]{1,0:T(8,128)S(1)} collective-permute-done((f32[584,128]{1,0:T(8,128)S(1)}, f32[584,128]{1,0:T(8,128)S(1)}, u32[]{:S(2)}, u32[]{:S(2)}) %collective-permute-start.1) | collective-permute-done | bytes 299040 | tf_op jit(solution)/shard_map/ppermute | solution.py:261
  32.5 0.0 collective-permute-start.2
  32.5 0.0 copy-start
  32.5 1.0 %copy-done = f32[2048,64]{0,1:T(8,128)S(1)} copy-done((f32[2048,64]{0,1:T(8,128)S(1)}, f32[2048,64]{0,1:T(8,128)}, u32[]{:S(2)}) %copy-start) | copy-done | bytes 524312
  33.6 3.9 %shard_map.65 = (bf16[2048,512]{1,0:T(8,128)(2,1)S(1)}, bf16[2048,512]{1,0:T(8,128)(2,1)S(1)}, bf16[512,2048]{1,0:T(8,128)(2,1)S(1)}, bf16[512,2048]{1,0:T(8,128)(2,1)S(1)}, bf16[2048,256]{1,0:T(8,128)(2,1)S(1)}) custom-call(f32[2048,512]{1,0:T(8,128)} %latent_hbm.3, f32[64,2048]{1,0:T(8,128)S(1)} %bitcast.1), custom_call_target="tpu_custom_call" | custom-call | flops 1000000000 | bytes 14155776 | tf_op jit(solution)/shard_map/pallas_call | solution.py:31
  37.5 0.0 collective-permute-done.5.refs_0_
  37.5 5.2 %collective-permute-start.8 = (f32[584,128]{1,0:T(8,128)S(1)}, f32[584,128]{1,0:T(8,128)S(1)}, u32[]{:S(2)}, u32[]{:S(2)}) collective-permute-start(f32[584,128]{1,0:T(8,128)S(1)} %collective-permute-done.5.refs_0_), channel_id=1, source_target_pairs={{2,4},{4,2},{6,8},{8,6},{10,12},{12,10},{14,16},{16,14},{18,20},{2... | collective-permute-start | bytes 897032 | tf_op jit(solution)/shard_map/ppermute | solution.py:261
  42.7 0.0 collective-permute-done.2.refs_0_
  42.7 3.2 %shard_map.67 = f32[520,128]{1,0:T(8,128)S(1)} custom-call(f32[584,128]{1,0:T(8,128)S(1)} %collective-permute-done.2.refs_0_, bf16[2048,512]{1,0:T(8,128)(2,1)S(1)} %get-tuple-element.14.refs_1_.refs_2_, bf16[2048,512]{1,0:T(8,128)(2,1)S(1)} %get-tuple-element.15.refs_2_.refs_3_, bf16[512,2048]{1,0:T(8,128)(2,1)S(1)} %get-tuple-element.16.refs_3_.refs_4_, ...), custom_call_target="tpu_custom_call" | custom-call | flops 3422552064 | bytes 10002432 | tf_op jit(solution)/shard_map/pallas_call | solution.py:31
  46.0 0.1 collective-permute-start.3
  46.1 2.3 %collective-permute-done.8.refs_0_ = f32[584,128]{1,0:T(8,128)S(1)} collective-permute-done((f32[584,128]{1,0:T(8,128)S(1)}, f32[584,128]{1,0:T(8,128)S(1)}, u32[]{:S(2)}, u32[]{:S(2)}) %collective-permute-start.8) | collective-permute-done | bytes 299040 | tf_op jit(solution)/shard_map/ppermute | solution.py:261
  48.5 3.2 %shard_map.72 = f32[520,128]{1,0:T(8,128)S(1)} custom-call(f32[584,128]{1,0:T(8,128)S(1)} %collective-permute-done.8.refs_0_, bf16[2048,512]{1,0:T(8,128)(2,1)S(1)} %get-tuple-element.14.refs_1_.refs_2_, bf16[2048,512]{1,0:T(8,128)(2,1)S(1)} %get-tuple-element.15.refs_2_.refs_3_, bf16[512,2048]{1,0:T(8,128)(2,1)S(1)} %get-tuple-element.16.refs_3_.refs_4_, ...), custom_call_target="tpu_custom_call" | custom-call | flops 3422552064 | bytes 10002432 | tf_op jit(solution)/shard_map/pallas_call | solution.py:31
  51.7 5.1 %collective-permute-start.9 = (f32[520,128]{1,0:T(8,128)S(1)}, f32[520,128]{1,0:T(8,128)S(1)}, u32[]{:S(2)}, u32[]{:S(2)}) collective-permute-start(f32[520,128]{1,0:T(8,128)S(1)} %shard_map.72), channel_id=1, source_target_pairs={{2,4},{4,2},{6,8},{8,6},{10,12},{12,10},{14,16},{16,14},{18,20},{2... | collective-permute-start | bytes 798728 | tf_op jit(solution)/shard_map/ppermute | solution.py:261
  56.8 4.5 %shard_map.68 = (f32[520,128]{1,0:T(8,128)S(1)}, f32[520,128]{1,0:T(8,128)S(1)}) custom-call(f32[584,128]{1,0:T(8,128)S(1)} %collective-permute-done.5.refs_0_, f32[584,128]{1,0:T(8,128)S(1)} %collective-permute-done.1.refs_1_, bf16[2048,512]{1,0:T(8,128)(2,1)S(1)} %get-tuple-element.14.refs_1_.refs_2_, ...), custom_call_target="tpu_custom_call" | custom-call | flops 6845104128 | bytes 10567680 | tf_op jit(solution)/shard_map/pallas_call | solution.py:31
  61.3 0.0 collective-permute-done.3.a
  61.3 0.1 shard_map.69
  61.4 0.7 collective-permute-start.6
  62.1 0.0 collective-permute-done.9.a
  62.1 0.1 shard_map.73
  62.1 0.0 copy-start.1
  62.1 0.1 collective-permute-start.10
  62.3 4.5 %shard_map.70 = (f32[520,128]{1,0:T(8,128)S(1)}, f32[520,128]{1,0:T(8,128)S(1)}) custom-call(f32[584,128]{1,0:T(8,128)S(1)} %collective-permute-done.refs_0_, f32[584,128]{1,0:T(8,128)S(1)} %collective-permute-done.4.refs_1_, bf16[2048,512]{1,0:T(8,128)(2,1)S(1)} %get-tuple-element.14.refs_1_.refs_2_, ...), custom_call_target="tpu_custom_call" | custom-call | flops 6845104128 | bytes 10567680 | tf_op jit(solution)/shard_map/pallas_call | solution.py:31
  66.8 4.4 %collective-permute-done.6.a = f32[520,128]{1,0:T(8,128)S(1)} collective-permute-done((f32[520,128]{1,0:T(8,128)S(1)}, f32[520,128]{1,0:T(8,128)S(1)}, u32[]{:S(2)}, u32[]{:S(2)}) %collective-permute-start.6) | collective-permute-done | bytes 266272 | tf_op jit(solution)/shard_map/ppermute | solution.py:261
  71.3 0.1 collective-permute-start.7
  71.4 0.0 collective-permute-done.10.a
  71.5 4.7 %collective-permute-start.11 = (f32[520,128]{1,0:T(8,128)S(1)}, f32[520,128]{1,0:T(8,128)S(1)}, u32[]{:S(2)}, u32[]{:S(2)}) collective-permute-start(f32[520,128]{1,0:T(8,128)S(1)} %shard_map.74), channel_id=1, source_target_pairs={{2,4},{4,2},{6,8},{8,6},{10,12},{12,10},{14,16},{16,14},{18,20},{2... | collective-permute-start | bytes 798728 | tf_op jit(solution)/shard_map/ppermute | solution.py:261
  76.2 0.0 copy-done.1
  76.2 3.2 %shard_map.66.a_ref = f32[520,128]{1,0:T(8,128)S(1)} custom-call(f32[584,128]{1,0:T(8,128)S(1)} %copy-done.1, bf16[2048,512]{1,0:T(8,128)(2,1)S(1)} %get-tuple-element.14.refs_1_.refs_2_, bf16[2048,512]{1,0:T(8,128)(2,1)S(1)} %get-tuple-element.15.refs_2_.refs_3_, bf16[512,2048]{1,0:T(8,128)(2,1)S(1)} %get-tuple-element.16.refs_3_.refs_4_, ...), custom_call_target="tpu_custom_call" | custom-call | flops 3422552064 | bytes 10002432 | tf_op jit(solution)/shard_map/pallas_call | solution.py:31
  79.4 0.0 collective-permute-done.7.b_ref
  79.4 1.9 %collective-permute-done.11.c_ref = f32[520,128]{1,0:T(8,128)S(1)} collective-permute-done((f32[520,128]{1,0:T(8,128)S(1)}, f32[520,128]{1,0:T(8,128)S(1)}, u32[]{:S(2)}, u32[]{:S(2)}) %collective-permute-start.11) | collective-permute-done | bytes 266272 | tf_op jit(solution)/shard_map/ppermute | solution.py:261
  81.4 0.9 %shard_map.75 = f32[2,64,512]{2,1,0:T(8,128)} custom-call(f32[520,128]{1,0:T(8,128)S(1)} %shard_map.66.a_ref, f32[520,128]{1,0:T(8,128)S(1)} %collective-permute-done.7.b_ref, f32[520,128]{1,0:T(8,128)S(1)} %collective-permute-done.11.c_ref), custom_call_target="tpu_custom_call" | custom-call | flops 1000000 | bytes 1060864 | tf_op jit(solution)/shard_map/pallas_call | solution.py:31
  (2 shorter events, 0.1 us)
Async XLA Ops:
  1.9 15.4 %collective-permute-start = (f32[584,128]{1,0:T(8,128)}, f32[584,128]{1,0:T(8,128)S(1)}, u32[]{:S(2)}, u32[]{:S(2)}) collective-permute-start(f32[584,128]{1,0:T(8,128)} %shard_map.64.refs_0_), channel_id=1, source_target_pairs={{0,2},{2,0},{4,6},{6,4},{8,10},{10,8},{12,14},{14,12},{16,18},{18,... | collective-permute-start | bytes 897032 | tf_op jit(solution)/shard_map/ppermute | solution.py:261
  4.8 21.5 %collective-permute-start.4 = (f32[584,128]{1,0:T(8,128)}, f32[584,128]{1,0:T(8,128)S(1)}, u32[]{:S(2)}, u32[]{:S(2)}) collective-permute-start(f32[584,128]{1,0:T(8,128)} %shard_map.64.refs_0_), channel_id=1, source_target_pairs={{2,4},{4,2},{6,8},{8,6},{10,12},{12,10},{14,16},{16,14},{18,20},{2... | collective-permute-start | bytes 897032 | tf_op jit(solution)/shard_map/ppermute | solution.py:261
  17.3 15.3 %collective-permute-start.1 = (f32[584,128]{1,0:T(8,128)S(1)}, f32[584,128]{1,0:T(8,128)S(1)}, u32[]{:S(2)}, u32[]{:S(2)}) collective-permute-start(f32[584,128]{1,0:T(8,128)S(1)} %collective-permute-done.refs_0_), channel_id=1, source_target_pairs={{2,4},{4,2},{6,8},{8,6},{10,12},{12,10},{14,16},{16,14},{18,20},{2... | collective-permute-start | bytes 897032 | tf_op jit(solution)/shard_map/ppermute | solution.py:261
  26.2 11.3 %collective-permute-start.5 = (f32[584,128]{1,0:T(8,128)S(1)}, f32[584,128]{1,0:T(8,128)S(1)}, u32[]{:S(2)}, u32[]{:S(2)}) collective-permute-start(f32[584,128]{1,0:T(8,128)S(1)} %collective-permute-done.4.refs_1_), channel_id=1, source_target_pairs={{0,2},{2,0},{4,6},{6,4},{8,10},{10,8},{12,14},{14,12},{16,18},{18,... | collective-permute-start | bytes 897032 | tf_op jit(solution)/shard_map/ppermute | solution.py:261
  32.5 10.2 %collective-permute-start.2 = (f32[584,128]{1,0:T(8,128)S(1)}, f32[584,128]{1,0:T(8,128)S(1)}, u32[]{:S(2)}, u32[]{:S(2)}) collective-permute-start(f32[584,128]{1,0:T(8,128)S(1)} %collective-permute-done.1.refs_1_), channel_id=1, source_target_pairs={{0,2},{2,0},{4,6},{6,4},{8,10},{10,8},{12,14},{14,12},{16,18},{18,... | collective-permute-start | bytes 897032 | tf_op jit(solution)/shard_map/ppermute | solution.py:261
  32.5 1.0 %copy-start = (f32[2048,64]{0,1:T(8,128)S(1)}, f32[2048,64]{0,1:T(8,128)}, u32[]{:S(2)}) copy-start(f32[2048,64]{0,1:T(8,128)} %param.9) | copy-start | bytes 1572868
  37.5 10.9 %collective-permute-start.8 = (f32[584,128]{1,0:T(8,128)S(1)}, f32[584,128]{1,0:T(8,128)S(1)}, u32[]{:S(2)}, u32[]{:S(2)}) collective-permute-start(f32[584,128]{1,0:T(8,128)S(1)} %collective-permute-done.5.refs_0_), channel_id=1, source_target_pairs={{2,4},{4,2},{6,8},{8,6},{10,12},{12,10},{14,16},{16,14},{18,20},{2... | collective-permute-start | bytes 897032 | tf_op jit(solution)/shard_map/ppermute | solution.py:261
  46.0 15.3 %collective-permute-start.3 = (f32[520,128]{1,0:T(8,128)S(1)}, f32[520,128]{1,0:T(8,128)S(1)}, u32[]{:S(2)}, u32[]{:S(2)}) collective-permute-start(f32[520,128]{1,0:T(8,128)S(1)} %shard_map.67), channel_id=1, source_target_pairs={{0,2},{2,0},{4,6},{6,4},{8,10},{10,8},{12,14},{14,12},{16,18},{18,... | collective-permute-start | bytes 798728 | tf_op jit(solution)/shard_map/ppermute | solution.py:261
  51.7 10.4 %collective-permute-start.9 = (f32[520,128]{1,0:T(8,128)S(1)}, f32[520,128]{1,0:T(8,128)S(1)}, u32[]{:S(2)}, u32[]{:S(2)}) collective-permute-start(f32[520,128]{1,0:T(8,128)S(1)} %shard_map.72), channel_id=1, source_target_pairs={{2,4},{4,2},{6,8},{8,6},{10,12},{12,10},{14,16},{16,14},{18,20},{2... | collective-permute-start | bytes 798728 | tf_op jit(solution)/shard_map/ppermute | solution.py:261
  61.4 9.9 %collective-permute-start.6 = (f32[520,128]{1,0:T(8,128)S(1)}, f32[520,128]{1,0:T(8,128)S(1)}, u32[]{:S(2)}, u32[]{:S(2)}) collective-permute-start(f32[520,128]{1,0:T(8,128)S(1)} %shard_map.69), channel_id=1, source_target_pairs={{2,4},{4,2},{6,8},{8,6},{10,12},{12,10},{14,16},{16,14},{18,20},{2... | collective-permute-start | bytes 798728 | tf_op jit(solution)/shard_map/ppermute | solution.py:261
  62.1 14.0 %copy-start.1 = (f32[584,128]{1,0:T(8,128)S(1)}, f32[584,128]{1,0:T(8,128)}, u32[]{:S(2)}) copy-start(f32[584,128]{1,0:T(8,128)} %shard_map.64.refs_0_) | copy-start | bytes 897028
  62.1 9.3 %collective-permute-start.10 = (f32[520,128]{1,0:T(8,128)S(1)}, f32[520,128]{1,0:T(8,128)S(1)}, u32[]{:S(2)}, u32[]{:S(2)}) collective-permute-start(f32[520,128]{1,0:T(8,128)S(1)} %shard_map.73), channel_id=1, source_target_pairs={{0,2},{2,0},{4,6},{6,4},{8,10},{10,8},{12,14},{14,12},{16,18},{18,... | collective-permute-start | bytes 798728 | tf_op jit(solution)/shard_map/ppermute | solution.py:261
  71.3 8.1 %collective-permute-start.7 = (f32[520,128]{1,0:T(8,128)S(1)}, f32[520,128]{1,0:T(8,128)S(1)}, u32[]{:S(2)}, u32[]{:S(2)}) collective-permute-start(f32[520,128]{1,0:T(8,128)S(1)} %shard_map.71), channel_id=1, source_target_pairs={{0,2},{2,0},{4,6},{6,4},{8,10},{10,8},{12,14},{14,12},{16,18},{18,... | collective-permute-start | bytes 798728 | tf_op jit(solution)/shard_map/ppermute | solution.py:261
  71.5 9.9 %collective-permute-start.11 = (f32[520,128]{1,0:T(8,128)S(1)}, f32[520,128]{1,0:T(8,128)S(1)}, u32[]{:S(2)}, u32[]{:S(2)}) collective-permute-start(f32[520,128]{1,0:T(8,128)S(1)} %shard_map.74), channel_id=1, source_target_pairs={{2,4},{4,2},{6,8},{8,6},{10,12},{12,10},{14,16},{16,14},{18,20},{2... | collective-permute-start | bytes 798728 | tf_op jit(solution)/shard_map/ppermute | solution.py:261

commit v2 on v1

--- a/solution.py
+++ b/solution.py
@@ -22,7 +22,7 @@
 BF16 = jnp.bfloat16
 
 VMEM = pl.BlockSpec(memory_space=pltpu.VMEM)
-HBM = pl.BlockSpec(memory_space=pltpu.HBM)
+ANY = pl.BlockSpec(memory_space=pl.ANY)
 
 
 def call(body, outs, in_specs, args, flops, scratch=(), limit=24):
@@ -37,6 +37,10 @@
         compiler_params=pltpu.CompilerParams(vmem_limit_bytes=limit * MIB),
         cost_estimate=pl.CostEstimate(flops=flops, bytes_accessed=nbytes, transcendentals=0),
     )(*args)
+
+
+def in_hbm(x):
+    return pltpu.with_memory_space_constraint(x, pltpu.HBM)
 
 
 def dot(a, b):
@@ -92,8 +96,8 @@
         pltpu.VMEM(q_rope.shape, F32),
         pltpu.SemaphoreType.DMA((4,)),
     ]
-    args = (home_offset, lengths, q_latent, q_rope)
-    return call(pack_body, out, [HBM] * 4, args, 1000, scratch, limit=57)[0]
+    args = tuple(in_hbm(x) for x in (home_offset, lengths, q_latent, q_rope))
+    return call(pack_body, out, [ANY] * 4, args, 1000, scratch)[0]
 
 
 def prepare_body(latent_hbm, rope_hbm, ch_ref, cl_ref, th_ref, tl_ref, kr_ref, latent_ref, rope_ref, sems):
@@ -135,8 +139,8 @@
         pltpu.VMEM((rope, cells), F32),
         pltpu.SemaphoreType.DMA((cells // 256 + 1,)),
     ]
-    args = (cache_latent, cache_rope.T)
-    return call(prepare_body, outs, [HBM] * 2, args, 10**9, scratch, limit=44)
+    args = (in_hbm(cache_latent), in_hbm(cache_rope.T))
+    return call(prepare_body, outs, [ANY] * 2, args, 10**9, scratch)
 
 
 def attend_body(hop, sides, *refs):
@@ -254,11 +258,13 @@
 
 
 def swap(x, parity):
-    size = lax.axis_size("blk")
+    size, cores = lax.axis_size("blk"), lax.axis_size("head")
     pairs = []
-    for i in range(parity, size + parity, 2):
-        pairs += [(i % size, (i + 1) % size), ((i + 1) % size, i % size)]
-    return lax.ppermute(x, "blk", pairs)
+    for core in range(cores):
+        for i in range(parity, size + parity, 2):
+            one, two = i % size * cores + core, (i + 1) % size * cores + core
+            pairs += [(one, two), (two, one)]
+    return lax.ppermute(x, ("blk", "head"), pairs)
 
 
 def shards(q_latent, q_rope, cache_latent, cache_rope, home_offset, lengths):

time: 82.4 us -> 80.5 us (0.977)
  local copies, waits for them, and re-layouts: 1.05 us -> 0 us
    unnamed x4 -> x0, local copies, waits for them, and re-layouts: 1.05 us -> none
  transfers between devices with their start and end apart: 12 -> 12, of which waited for: 4 -> 4; matrix products, arithmetic and copies ran while one was open for 0% -> 0% of each run, Pallas kernels for 28% -> 29%
where the time goes in v2:
time: 80.5 us; the launch traced here: 80.4 us
  starting transfers between devices  39.8 us (49%)
  Pallas kernels  25 us (31%)
  waiting for transfers between devices  15.4 us (19%)
    ppermute x12, starting transfers between devices, swap(): return lax.ppermute(x, ('blk', 'head'), pairs)  39.8 us
    pallas_call x12, Pallas kernels, call(): pl.pallas_call(body, out_shape=outs, in_specs=in_specs, out_specs=[VMEM]...  25 us
    ppermute x12, waiting for transfers between devices, swap(): return lax.ppermute(x, ('blk', 'head'), pairs)  15.4 us
  transfers between devices with their start and end apart: 12, of which 4 were waited for; matrix products, arithmetic and copies ran while one was open for 0% of the time, Pallas kernels for 29%

profile of v2, /device:TPU:640, one launch (start us, length us, event | category | flops | bytes accessed | tf_op | source)
XLA Modules:
  0.0 80.4 jit_solution(15087861165062392690)
XLA Ops:
  0.0 1.2 %shard_map.64.refs_0_ = f32[584,128]{1,0:T(8,128)S(1)} custom-call(s32[2]{0:T(128)} %home_hbm.1, s32[2]{0:T(128)} %lengths_hbm.1, f32[2,64,512]{2,1,0:T(8,128)} %latent_hbm.2, f32[2,64,64]{2,1,0:T(8,128)} %rope_hbm.1), custom_call_target="tpu_custom_call" | custom-call | flops 1000 | bytes 593936 | tf_op jit(solution)/shard_map/pallas_call | solution.py:31
  1.2 2.9 %collective-permute-start = (f32[584,128]{1,0:T(8,128)S(1)}, f32[584,128]{1,0:T(8,128)S(1)}, u32[]{:S(2)}, u32[]{:S(2)}) collective-permute-start(f32[584,128]{1,0:T(8,128)S(1)} %shard_map.64.refs_0_), channel_id=1, source_target_pairs={{0,2},{2,0},{4,6},{6,4},{8,10},{10,8},{12,14},{14,12},{16,18},{18,... | collective-permute-start | bytes 897032 | tf_op jit(solution)/shard_map/ppermute | solution.py:267
  4.1 12.5 %collective-permute-start.4 = (f32[584,128]{1,0:T(8,128)S(1)}, f32[584,128]{1,0:T(8,128)S(1)}, u32[]{:S(2)}, u32[]{:S(2)}) collective-permute-start(f32[584,128]{1,0:T(8,128)S(1)} %shard_map.64.refs_0_), channel_id=1, source_target_pairs={{2,4},{4,2},{6,8},{8,6},{10,12},{12,10},{14,16},{16,14},{18,20},{2... | collective-permute-start | bytes 897032 | tf_op jit(solution)/shard_map/ppermute | solution.py:267
  16.6 0.0 collective-permute-done.refs_0_
  16.6 8.8 %collective-permute-start.1 = (f32[584,128]{1,0:T(8,128)S(1)}, f32[584,128]{1,0:T(8,128)S(1)}, u32[]{:S(2)}, u32[]{:S(2)}) collective-permute-start(f32[584,128]{1,0:T(8,128)S(1)} %collective-permute-done.refs_0_), channel_id=1, source_target_pairs={{2,4},{4,2},{6,8},{8,6},{10,12},{12,10},{14,16},{16,14},{18,20},{2... | collective-permute-start | bytes 897032 | tf_op jit(solution)/shard_map/ppermute | solution.py:267
  25.3 0.0 collective-permute-done.4.refs_1_
  25.3 0.0 collective-permute-start.5
  25.3 6.3 %collective-permute-done.1.refs_1_ = f32[584,128]{1,0:T(8,128)S(1)} collective-permute-done((f32[584,128]{1,0:T(8,128)S(1)}, f32[584,128]{1,0:T(8,128)S(1)}, u32[]{:S(2)}, u32[]{:S(2)}) %collective-permute-start.1) | collective-permute-done | bytes 299040 | tf_op jit(solution)/shard_map/ppermute | solution.py:267
  31.6 0.0 collective-permute-start.2
  31.6 4.1 %shard_map.65 = (bf16[2048,512]{1,0:T(8,128)(2,1)S(1)}, bf16[2048,512]{1,0:T(8,128)(2,1)S(1)}, bf16[512,2048]{1,0:T(8,128)(2,1)S(1)}, bf16[512,2048]{1,0:T(8,128)(2,1)S(1)}, bf16[2048,256]{1,0:T(8,128)(2,1)S(1)}) custom-call(f32[2048,512]{1,0:T(8,128)} %latent_hbm.3, f32[64,2048]{1,0:T(8,128)} %bitcast.1), custom_call_target="tpu_custom_call" | custom-call | flops 1000000000 | bytes 14155776 | tf_op jit(solution)/shard_map/pallas_call | solution.py:31
  35.7 0.0 collective-permute-done.5.refs_0_
  35.7 5.2 %collective-permute-start.8 = (f32[584,128]{1,0:T(8,128)S(1)}, f32[584,128]{1,0:T(8,128)S(1)}, u32[]{:S(2)}, u32[]{:S(2)}) collective-permute-start(f32[584,128]{1,0:T(8,128)S(1)} %collective-permute-done.5.refs_0_), channel_id=1, source_target_pairs={{2,4},{4,2},{6,8},{8,6},{10,12},{12,10},{14,16},{16,14},{18,20},{2... | collective-permute-start | bytes 897032 | tf_op jit(solution)/shard_map/ppermute | solution.py:267
  40.9 0.0 collective-permute-done.2.refs_0_
  40.9 3.2 %shard_map.67 = f32[520,128]{1,0:T(8,128)S(1)} custom-call(f32[584,128]{1,0:T(8,128)S(1)} %collective-permute-done.2.refs_0_, bf16[2048,512]{1,0:T(8,128)(2,1)S(1)} %get-tuple-element.14.refs_1_.refs_2_, bf16[2048,512]{1,0:T(8,128)(2,1)S(1)} %get-tuple-element.15.refs_2_.refs_3_, bf16[512,2048]{1,0:T(8,128)(2,1)S(1)} %get-tuple-element.16.refs_3_.refs_4_, ...), custom_call_target="tpu_custom_call" | custom-call | flops 3422552064 | bytes 10002432 | tf_op jit(solution)/shard_map/pallas_call | solution.py:31
  44.1 0.1 collective-permute-start.3
  44.3 2.3 %collective-permute-done.8.refs_0_ = f32[584,128]{1,0:T(8,128)S(1)} collective-permute-done((f32[584,128]{1,0:T(8,128)S(1)}, f32[584,128]{1,0:T(8,128)S(1)}, u32[]{:S(2)}, u32[]{:S(2)}) %collective-permute-start.8) | collective-permute-done | bytes 299040 | tf_op jit(solution)/shard_map/ppermute | solution.py:267
  46.6 3.2 %shard_map.72 = f32[520,128]{1,0:T(8,128)S(1)} custom-call(f32[584,128]{1,0:T(8,128)S(1)} %collective-permute-done.8.refs_0_, bf16[2048,512]{1,0:T(8,128)(2,1)S(1)} %get-tuple-element.14.refs_1_.refs_2_, bf16[2048,512]{1,0:T(8,128)(2,1)S(1)} %get-tuple-element.15.refs_2_.refs_3_, bf16[512,2048]{1,0:T(8,128)(2,1)S(1)} %get-tuple-element.16.refs_3_.refs_4_, ...), custom_call_target="tpu_custom_call" | custom-call | flops 3422552064 | bytes 10002432 | tf_op jit(solution)/shard_map/pallas_call | solution.py:31
  49.9 4.9 %collective-permute-start.9 = (f32[520,128]{1,0:T(8,128)S(1)}, f32[520,128]{1,0:T(8,128)S(1)}, u32[]{:S(2)}, u32[]{:S(2)}) collective-permute-start(f32[520,128]{1,0:T(8,128)S(1)} %shard_map.72), channel_id=1, source_target_pairs={{2,4},{4,2},{6,8},{8,6},{10,12},{12,10},{14,16},{16,14},{18,20},{2... | collective-permute-start | bytes 798728 | tf_op jit(solution)/shard_map/ppermute | solution.py:267
  54.8 4.5 %shard_map.68 = (f32[520,128]{1,0:T(8,128)S(1)}, f32[520,128]{1,0:T(8,128)S(1)}) custom-call(f32[584,128]{1,0:T(8,128)S(1)} %collective-permute-done.5.refs_0_, f32[584,128]{1,0:T(8,128)S(1)} %collective-permute-done.1.refs_1_, bf16[2048,512]{1,0:T(8,128)(2,1)S(1)} %get-tuple-element.14.refs_1_.refs_2_, ...), custom_call_target="tpu_custom_call" | custom-call | flops 6845104128 | bytes 10567680 | tf_op jit(solution)/shard_map/pallas_call | solution.py:31
  59.3 0.0 collective-permute-done.3.a
  59.3 0.9 %collective-permute-start.6 = (f32[520,128]{1,0:T(8,128)S(1)}, f32[520,128]{1,0:T(8,128)S(1)}, u32[]{:S(2)}, u32[]{:S(2)}) collective-permute-start(f32[520,128]{1,0:T(8,128)S(1)} %shard_map.69), channel_id=1, source_target_pairs={{2,4},{4,2},{6,8},{8,6},{10,12},{12,10},{14,16},{16,14},{18,20},{2... | collective-permute-start | bytes 798728 | tf_op jit(solution)/shard_map/ppermute | solution.py:267
  60.2 0.0 collective-permute-done.9.a
  60.3 0.1 collective-permute-start.10
  60.4 4.5 %shard_map.70 = (f32[520,128]{1,0:T(8,128)S(1)}, f32[520,128]{1,0:T(8,128)S(1)}) custom-call(f32[584,128]{1,0:T(8,128)S(1)} %collective-permute-done.refs_0_, f32[584,128]{1,0:T(8,128)S(1)} %collective-permute-done.4.refs_1_, bf16[2048,512]{1,0:T(8,128)(2,1)S(1)} %get-tuple-element.14.refs_1_.refs_2_, ...), custom_call_target="tpu_custom_call" | custom-call | flops 6845104128 | bytes 10567680 | tf_op jit(solution)/shard_map/pallas_call | solution.py:31
  64.9 4.5 %collective-permute-done.6.a = f32[520,128]{1,0:T(8,128)S(1)} collective-permute-done((f32[520,128]{1,0:T(8,128)S(1)}, f32[520,128]{1,0:T(8,128)S(1)}, u32[]{:S(2)}, u32[]{:S(2)}) %collective-permute-start.6) | collective-permute-done | bytes 266272 | tf_op jit(solution)/shard_map/ppermute | solution.py:267
  69.4 0.1 shard_map.71
  69.4 0.1 collective-permute-start.7
  69.6 0.0 collective-permute-done.10.a
  69.6 0.1 shard_map.74
  69.7 4.3 %collective-permute-start.11 = (f32[520,128]{1,0:T(8,128)S(1)}, f32[520,128]{1,0:T(8,128)S(1)}, u32[]{:S(2)}, u32[]{:S(2)}) collective-permute-start(f32[520,128]{1,0:T(8,128)S(1)} %shard_map.74), channel_id=1, source_target_pairs={{2,4},{4,2},{6,8},{8,6},{10,12},{12,10},{14,16},{16,14},{18,20},{2... | collective-permute-start | bytes 798728 | tf_op jit(solution)/shard_map/ppermute | solution.py:267
  73.9 3.2 %shard_map.66.a_ref = f32[520,128]{1,0:T(8,128)S(1)} custom-call(f32[584,128]{1,0:T(8,128)S(1)} %shard_map.64.refs_0_, bf16[2048,512]{1,0:T(8,128)(2,1)S(1)} %get-tuple-element.14.refs_1_.refs_2_, bf16[2048,512]{1,0:T(8,128)(2,1)S(1)} %get-tuple-element.15.refs_2_.refs_3_, bf16[512,2048]{1,0:T(8,128)(2,1)S(1)} %get-tuple-element.16.refs_3_.refs_4_, ...), custom_call_target="tpu_custom_call" | custom-call | flops 3422552064 | bytes 10002432 | tf_op jit(solution)/shard_map/pallas_call | solution.py:31
  77.2 0.0 collective-permute-done.7.b_ref
  77.2 2.3 %collective-permute-done.11.c_ref = f32[520,128]{1,0:T(8,128)S(1)} collective-permute-done((f32[520,128]{1,0:T(8,128)S(1)}, f32[520,128]{1,0:T(8,128)S(1)}, u32[]{:S(2)}, u32[]{:S(2)}) %collective-permute-start.11) | collective-permute-done | bytes 266272 | tf_op jit(solution)/shard_map/ppermute | solution.py:267
  79.5 0.9 %shard_map.75 = f32[2,64,512]{2,1,0:T(8,128)} custom-call(f32[520,128]{1,0:T(8,128)S(1)} %shard_map.66.a_ref, f32[520,128]{1,0:T(8,128)S(1)} %collective-permute-done.7.b_ref, f32[520,128]{1,0:T(8,128)S(1)} %collective-permute-done.11.c_ref), custom_call_target="tpu_custom_call" | custom-call | flops 1000000 | bytes 1060864 | tf_op jit(solution)/shard_map/pallas_call | solution.py:31
  (2 shorter events, 0.1 us)
Async XLA Ops:
  1.2 15.4 %collective-permute-start = (f32[584,128]{1,0:T(8,128)S(1)}, f32[584,128]{1,0:T(8,128)S(1)}, u32[]{:S(2)}, u32[]{:S(2)}) collective-permute-start(f32[584,128]{1,0:T(8,128)S(1)} %shard_map.64.refs_0_), channel_id=1, source_target_pairs={{0,2},{2,0},{4,6},{6,4},{8,10},{10,8},{12,14},{14,12},{16,18},{18,... | collective-permute-start | bytes 897032 | tf_op jit(solution)/shard_map/ppermute | solution.py:267
  4.1 21.3 %collective-permute-start.4 = (f32[584,128]{1,0:T(8,128)S(1)}, f32[584,128]{1,0:T(8,128)S(1)}, u32[]{:S(2)}, u32[]{:S(2)}) collective-permute-start(f32[584,128]{1,0:T(8,128)S(1)} %shard_map.64.refs_0_), channel_id=1, source_target_pairs={{2,4},{4,2},{6,8},{8,6},{10,12},{12,10},{14,16},{16,14},{18,20},{2... | collective-permute-start | bytes 897032 | tf_op jit(solution)/shard_map/ppermute | solution.py:267
  16.6 15.1 %collective-permute-start.1 = (f32[584,128]{1,0:T(8,128)S(1)}, f32[584,128]{1,0:T(8,128)S(1)}, u32[]{:S(2)}, u32[]{:S(2)}) collective-permute-start(f32[584,128]{1,0:T(8,128)S(1)} %collective-permute-done.refs_0_), channel_id=1, source_target_pairs={{2,4},{4,2},{6,8},{8,6},{10,12},{12,10},{14,16},{16,14},{18,20},{2... | collective-permute-start | bytes 897032 | tf_op jit(solution)/shard_map/ppermute | solution.py:267
  25.3 10.4 %collective-permute-start.5 = (f32[584,128]{1,0:T(8,128)S(1)}, f32[584,128]{1,0:T(8,128)S(1)}, u32[]{:S(2)}, u32[]{:S(2)}) collective-permute-start(f32[584,128]{1,0:T(8,128)S(1)} %collective-permute-done.4.refs_1_), channel_id=1, source_target_pairs={{0,2},{2,0},{4,6},{6,4},{8,10},{10,8},{12,14},{14,12},{16,18},{18,... | collective-permute-start | bytes 897032 | tf_op jit(solution)/shard_map/ppermute | solution.py:267
  31.6 9.3 %collective-permute-start.2 = (f32[584,128]{1,0:T(8,128)S(1)}, f32[584,128]{1,0:T(8,128)S(1)}, u32[]{:S(2)}, u32[]{:S(2)}) collective-permute-start(f32[584,128]{1,0:T(8,128)S(1)} %collective-permute-done.1.refs_1_), channel_id=1, source_target_pairs={{0,2},{2,0},{4,6},{6,4},{8,10},{10,8},{12,14},{14,12},{16,18},{18,... | collective-permute-start | bytes 897032 | tf_op jit(solution)/shard_map/ppermute | solution.py:267
  35.7 10.9 %collective-permute-start.8 = (f32[584,128]{1,0:T(8,128)S(1)}, f32[584,128]{1,0:T(8,128)S(1)}, u32[]{:S(2)}, u32[]{:S(2)}) collective-permute-start(f32[584,128]{1,0:T(8,128)S(1)} %collective-permute-done.5.refs_0_), channel_id=1, source_target_pairs={{2,4},{4,2},{6,8},{8,6},{10,12},{12,10},{14,16},{16,14},{18,20},{2... | collective-permute-start | bytes 897032 | tf_op jit(solution)/shard_map/ppermute | solution.py:267
  44.1 15.2 %collective-permute-start.3 = (f32[520,128]{1,0:T(8,128)S(1)}, f32[520,128]{1,0:T(8,128)S(1)}, u32[]{:S(2)}, u32[]{:S(2)}) collective-permute-start(f32[520,128]{1,0:T(8,128)S(1)} %shard_map.67), channel_id=1, source_target_pairs={{0,2},{2,0},{4,6},{6,4},{8,10},{10,8},{12,14},{14,12},{16,18},{18,... | collective-permute-start | bytes 798728 | tf_op jit(solution)/shard_map/ppermute | solution.py:267
  49.9 10.3 %collective-permute-start.9 = (f32[520,128]{1,0:T(8,128)S(1)}, f32[520,128]{1,0:T(8,128)S(1)}, u32[]{:S(2)}, u32[]{:S(2)}) collective-permute-start(f32[520,128]{1,0:T(8,128)S(1)} %shard_map.72), channel_id=1, source_target_pairs={{2,4},{4,2},{6,8},{8,6},{10,12},{12,10},{14,16},{16,14},{18,20},{2... | collective-permute-start | bytes 798728 | tf_op jit(solution)/shard_map/ppermute | solution.py:267
  59.3 10.0 %collective-permute-start.6 = (f32[520,128]{1,0:T(8,128)S(1)}, f32[520,128]{1,0:T(8,128)S(1)}, u32[]{:S(2)}, u32[]{:S(2)}) collective-permute-start(f32[520,128]{1,0:T(8,128)S(1)} %shard_map.69), channel_id=1, source_target_pairs={{2,4},{4,2},{6,8},{8,6},{10,12},{12,10},{14,16},{16,14},{18,20},{2... | collective-permute-start | bytes 798728 | tf_op jit(solution)/shard_map/ppermute | solution.py:267
  60.3 9.3 %collective-permute-start.10 = (f32[520,128]{1,0:T(8,128)S(1)}, f32[520,128]{1,0:T(8,128)S(1)}, u32[]{:S(2)}, u32[]{:S(2)}) collective-permute-start(f32[520,128]{1,0:T(8,128)S(1)} %shard_map.73), channel_id=1, source_target_pairs={{0,2},{2,0},{4,6},{6,4},{8,10},{10,8},{12,14},{14,12},{16,18},{18,... | collective-permute-start | bytes 798728 | tf_op jit(solution)/shard_map/ppermute | solution.py:267
  69.4 7.8 %collective-permute-start.7 = (f32[520,128]{1,0:T(8,128)S(1)}, f32[520,128]{1,0:T(8,128)S(1)}, u32[]{:S(2)}, u32[]{:S(2)}) collective-permute-start(f32[520,128]{1,0:T(8,128)S(1)} %shard_map.71), channel_id=1, source_target_pairs={{0,2},{2,0},{4,6},{6,4},{8,10},{10,8},{12,14},{14,12},{16,18},{18,... | collective-permute-start | bytes 798728 | tf_op jit(solution)/shard_map/ppermute | solution.py:267
  69.7 9.9 %collective-permute-start.11 = (f32[520,128]{1,0:T(8,128)S(1)}, f32[520,128]{1,0:T(8,128)S(1)}, u32[]{:S(2)}, u32[]{:S(2)}) collective-permute-start(f32[520,128]{1,0:T(8,128)S(1)} %shard_map.74), channel_id=1, source_target_pairs={{2,4},{4,2},{6,8},{8,6},{10,12},{12,10},{14,16},{16,14},{18,20},{2... | collective-permute-start | bytes 798728 | tf_op jit(solution)/shard_map/ppermute | solution.py:267
